TPU v7x, 32 devices: a whole 2x2x4 slice. The times are simulated.
32 devices in a mesh: dom: 16 (over z, x, core), grp: 2 (over y).
Axes of the slice: x: 2, y: 2, z: 4, core: 2. Of those that a mesh axis runs over, the one named last changes fastest.
Arguments:
- positions: float32 [3, 2, 16384], P(None, 'grp', 'dom'), as said below
- species: int32 [2, 16384], P('grp', 'dom'), may hold values from 0 to 3
- neighbours: int32 [48, 2, 16384], P(None, 'grp', 'dom'), may hold values from 0 to 16383, as said below
- slot_counts: int32 [2, 16384], P('grp', 'dom'), may hold values from 20 to 48, as said below
- structure: int32 [2, 16384], P('grp', 'dom'), may hold values from 0 to 511, as said below
- target_energy: float32 [2, 512], P('grp'), may hold values from -6 to 6
- radial_one: float32 [10, 12], replicated, may hold values from -6 to 6
- coupling_one: bfloat16 [4, 1960, 512], replicated, may hold values from -0.3125 to 0.3125
- coefficient_one: float32 [4, 512], replicated, may hold values from -0.25 to 0.25
- mixing: float32 [512, 4], replicated, may hold values from -0.375 to 0.375
- radial_two: float32 [10, 12], replicated, may hold values from -6 to 6
- coupling_two: bfloat16 [4, 1960, 512], replicated, may hold values from -0.3125 to 0.3125
- coefficient_two: float32 [4, 512], replicated, may hold values from -0.25 to 0.25
Outputs:
- energies: float32 [2, 512], P('grp')
- offsets: float32 [4], replicated
- forces: float32 [3, 2, 16384], P(None, 'grp', 'dom')
- radial_first: float32 [10, 12], replicated
- coefficient_first: float32 [4, 512], replicated
- mixing_gradient: float32 [512, 4], replicated
- radial_second: float32 [10, 12], replicated
- coefficient_second: float32 [4, 512], replicated
Inputs may be any that keep to these rules, and one draw needn't show every extreme that they name: Atoms of one structure are consecutive within a group; structure numbers start at 0 in each group and rise by one, and every group holds exactly 512 structures; each structure holds a multiple of 8 atoms, from 8 to 4096. `neighbours`: each slot names another atom of the same structure; it lies in the same block of 1024 consecutive atoms of the group as the atom or in an adjacent block. An atom may be named in several slots of one atom. Slots k < slot_counts are live, the others are ignored. `positions`: any two atoms of one structure are 0.9 or more apart.
All inputs are finite; a program needn't handle non-finite values.
Results may differ from a plain program's by a relative error of at most 0.0085.
The roundings to bfloat16 on the way count: a program that leaves them out, or rounds other values in their place, can miss the bound.
Values sent between devices are 32-bit elements; how exact they have to be, the bound alone decides.
A program may use at most 320 MiB of HBM per device.

v0:
```python
from functools import reduce
import math

import jax
import jax.numpy as jnp
from jax import lax
from jax.sharding import PartitionSpec as P

NRAD = 12
LMAX = 6
SPECIES = 4
NBR = 48


cutoff_radius = 5.0
density_scale = 0.17
norm_eps = 1e-05
ridge_weight = 0.1
highest = lax.Precision.HIGHEST


def with_halo(cells, sides, width):
    for axis, dim in sides:
        count = lax.axis_size(axis)
        ends = count - 1
        head = lax.slice_in_dim(cells, 0, width, axis=dim)
        tail = lax.slice_in_dim(cells, cells.shape[dim] - width, cells.shape[dim], axis=dim)
        cells = jnp.concatenate(
            [
                lax.ppermute(tail, axis, [(i, (i + 1) % count) for i in range(ends)]),
                cells,
                lax.ppermute(head, axis, [((i + 1) % count, i) for i in range(ends)]),
            ],
            axis=dim,
        )
    return cells


def double_factorial(number):
    result = 1.0
    while number > 1:
        result = result * number
        number = number - 2
    return result


def harmonics(unit_vec):
    coord_x, coord_y, coord_z = (unit_vec[0], unit_vec[1], unit_vec[2])
    cosines = [jnp.ones_like(coord_x)]
    sine_terms = [jnp.zeros_like(coord_x)]
    for degree in range(1, LMAX + 1):
        cosines.append(cosines[-1] * coord_x - sine_terms[-1] * coord_y)
        sine_terms.append(sine_terms[-1] * coord_x + cosines[-2] * coord_y)
    legendre = {}
    for azimuth in range(LMAX + 1):
        legendre[azimuth, azimuth] = jnp.full_like(coord_z, double_factorial(2 * azimuth - 1))
        if azimuth + 1 <= LMAX:
            legendre[azimuth + 1, azimuth] = (
                (2 * azimuth + 1) * coord_z * legendre[azimuth, azimuth]
            )
        for degree in range(azimuth + 2, LMAX + 1):
            legendre[degree, azimuth] = (
                (2 * degree - 1) * coord_z * legendre[degree - 1, azimuth]
                - (degree + azimuth - 1) * legendre[degree - 2, azimuth]
            ) / (degree - azimuth)
    columns = []
    for degree in range(LMAX + 1):
        for signed in range(-degree, degree + 1):
            azimuth = abs(signed)
            factor = math.sqrt(
                (2 * degree + 1)
                / (4 * math.pi)
                * math.factorial(degree - azimuth)
                / math.factorial(degree + azimuth)
            )
            scaled_poly = factor * legendre[degree, azimuth]
            if signed == 0:
                columns.append(scaled_poly)
            elif signed > 0:
                columns.append(math.sqrt(2.0) * scaled_poly * cosines[azimuth])
            else:
                columns.append(math.sqrt(2.0) * scaled_poly * sine_terms[azimuth])
    return jnp.stack(columns)


def radial_basis(distance, radial_weight):
    scaled = 2.0 * distance / cutoff_radius - 1.0
    cutoff = jnp.where(
        distance < cutoff_radius, 0.5 * (jnp.cos(jnp.pi * distance / cutoff_radius) + 1.0), 0.0
    )
    cheb_terms = [jnp.ones_like(scaled), scaled]
    for degree in range(2, NRAD):
        cheb_terms.append(2.0 * scaled * cheb_terms[-1] - cheb_terms[-2])
    cheb_basis = jnp.stack(cheb_terms[:NRAD])
    return jnp.einsum("np,pka->nka", radial_weight, cheb_basis, precision=highest) * cutoff


def densities(centres, neighbour_sites, channel_weight, live_slots, radial_weight):
    offsets_vec = neighbour_sites - centres[:, None, :]
    distance = jnp.sqrt(jnp.sum(offsets_vec * offsets_vec, axis=0))
    unit_vec = offsets_vec / distance
    radial = radial_basis(distance, radial_weight)
    angular = harmonics(unit_vec)
    weighted = channel_weight * (live_slots * density_scale)
    mixed_terms = (weighted[:, None] * radial[None]).reshape(-1, radial.shape[1], radial.shape[2])
    dens_out = jnp.einsum("mka,lka->mla", mixed_terms, angular, precision=highest)
    return dens_out.reshape(-1, dens_out.shape[-1])


def feature_map(invariants, mixing):
    inverse_rms = lax.rsqrt(jnp.mean(invariants * invariants, axis=0) + norm_eps)
    return jnp.einsum("qk,qa->ka", mixing, invariants, precision=highest) * inverse_rms


def small_solve(matrix, vector):
    order_n = matrix.shape[0]
    rows_now = [matrix[row_at] for row_at in range(order_n)]
    rights_now = [vector[row_at] for row_at in range(order_n)]
    for pivot_at in range(order_n):
        for below_at in range(pivot_at + 1, order_n):
            ratio_now = rows_now[below_at][pivot_at] / rows_now[pivot_at][pivot_at]
            rows_now[below_at] = rows_now[below_at] - ratio_now * rows_now[pivot_at]
            rights_now[below_at] = rights_now[below_at] - ratio_now * rights_now[pivot_at]
    answer = [None] * order_n
    for row_at in range(order_n - 1, -1, -1):
        running = rights_now[row_at]
        for later_at in range(row_at + 1, order_n):
            running = running - rows_now[row_at][later_at] * answer[later_at]
        answer[row_at] = running / rows_now[row_at][row_at]
    return jnp.stack(answer)


def contract(dens_in, coupling):
    factors = jnp.einsum(
        "vdq,da->vqa", coupling, dens_in.astype(jnp.bfloat16), preferred_element_type=jnp.float32
    )
    product = reduce(
        lambda earlier, later: earlier * later,
        [factors[index_v] for index_v in range(factors.shape[0])],
    )
    return (factors, product)


def contract_back(factors, upstream, coupling):
    partials = []
    for factor_at in range(factors.shape[0]):
        others = upstream
        for partner in range(factors.shape[0]):
            if partner != factor_at:
                others = others * factors[partner]
        partials.append(others)
    rounded = jnp.stack(partials).astype(jnp.bfloat16)
    return jnp.einsum("vdq,vqa->da", coupling, rounded, preferred_element_type=jnp.float32)


def ghost_pair(extended, width):
    return jnp.concatenate([extended[:, :width], extended[:, 2 * width :]], axis=1)


def owner_sum(extended, received, width):
    return extended[:, width : 2 * width] + received[:, :width] + received[:, 3 * width :]


def per_device(
    positions,
    species,
    neighbours,
    slot_counts,
    structure,
    target_energy,
    radial_one,
    coupling_one,
    coefficient_one,
    mixing,
    radial_two,
    coupling_two,
    coefficient_two,
):
    atoms_dev = positions.shape[2]
    centres = positions[:, 0, :]
    own_species = species[0]
    slot_index = neighbours[:, 0, :] - (lax.axis_index("dom") - 1) * atoms_dev
    live_slots = (jnp.arange(NBR, dtype=jnp.int32)[:, None] < slot_counts[0][None, :]).astype(
        jnp.float32
    )
    labels = jnp.arange(SPECIES, dtype=jnp.int32)
    onehot = (own_species[None, :] == labels[:, None]).astype(jnp.float32)
    sites_ext, species_ext = (
        with_halo(centres, (("dom", 1),), atoms_dev),
        with_halo(own_species.astype(jnp.float32)[None, :], (("dom", 1),), atoms_dev),
    )
    onehot_ext = (species_ext == labels[:, None].astype(jnp.float32)).astype(jnp.float32)

    def layer_density(sites_all, weights_all, radial_weight):
        middle = sites_all[:, atoms_dev : 2 * atoms_dev]
        return densities(
            middle, sites_all[:, slot_index], weights_all[:, slot_index], live_slots, radial_weight
        )

    dens_one, dens_one_back = jax.vjp(
        lambda sites_all, radial_weight: layer_density(sites_all, onehot_ext, radial_weight),
        sites_ext,
        radial_one,
    )
    factors_one, invariants_one = contract(dens_one, coupling_one)
    chosen_one = jnp.dot(coefficient_one.T, onehot, precision=highest)
    energy_one = jnp.sum(invariants_one * chosen_one, axis=0)
    features, features_back = jax.vjp(feature_map, invariants_one, mixing)
    features_ext = with_halo(features, (("dom", 1),), atoms_dev)
    dens_two, dens_two_back = jax.vjp(layer_density, sites_ext, features_ext, radial_two)
    factors_two, invariants_two = contract(dens_two, coupling_two)
    chosen_two = jnp.dot(coefficient_two.T, onehot, precision=highest)
    site_energy = energy_one + jnp.sum(invariants_two * chosen_two, axis=0)
    structure_ids = structure[0]
    slots_total = target_energy.shape[1]
    energy_part = jax.ops.segment_sum(site_energy, structure_ids, num_segments=slots_total)
    count_part = jax.ops.segment_sum(onehot.T, structure_ids, num_segments=slots_total)
    energy_sum, species_count = lax.psum((energy_part, count_part), "dom")
    atom_total = jnp.maximum(jnp.sum(species_count, axis=1), 1.0)
    fraction = species_count / atom_total[:, None]
    gram_part = jnp.dot(fraction.T, fraction, precision=highest)
    right_part = jnp.dot(fraction.T, target_energy[0], precision=highest)
    gram_matrix, right_side = lax.psum((gram_part, right_part), "grp")
    offsets = small_solve(
        gram_matrix + ridge_weight * jnp.eye(SPECIES, dtype=jnp.float32), right_side
    )
    energies = energy_sum / atom_total + jnp.dot(fraction, offsets, precision=highest)
    grad_dens_two = contract_back(factors_two, chosen_two, coupling_two)
    grad_sites_two, grad_features_ext, radial_second = dens_two_back(grad_dens_two)
    coefficient_second = jnp.dot(onehot, invariants_two.T, precision=highest)
    back_features = with_halo(ghost_pair(grad_features_ext, atoms_dev), (("dom", 1),), atoms_dev)
    grad_features = owner_sum(grad_features_ext, back_features, atoms_dev)
    settled = jnp.zeros_like(centres)
    grad_invariants, mixing_gradient = features_back(grad_features)
    grad_dens_one = contract_back(factors_one, chosen_one + grad_invariants, coupling_one)
    grad_sites_one, radial_first = dens_one_back(grad_dens_one)
    coefficient_first = jnp.dot(onehot, invariants_one.T, precision=highest)
    pending = grad_sites_one + grad_sites_two
    received = with_halo(ghost_pair(pending, atoms_dev), (("dom", 1),), atoms_dev)
    forces = -(owner_sum(pending, received, atoms_dev) + settled)
    radial_first, coefficient_first, mixing_gradient, radial_second, coefficient_second = lax.psum(
        (radial_first, coefficient_first, mixing_gradient, radial_second, coefficient_second),
        ("dom", "grp"),
    )
    return (
        energies[None, :],
        offsets,
        forces[:, None, :],
        radial_first,
        coefficient_first,
        mixing_gradient,
        radial_second,
        coefficient_second,
    )


def solution(mesh):
    in_specs = (
        P(None, "grp", "dom"),
        P("grp", "dom"),
        P(None, "grp", "dom"),
        P("grp", "dom"),
        P("grp", "dom"),
        P("grp", None),
        P(),
        P(),
        P(),
        P(),
        P(),
        P(),
        P(),
    )
    out_specs = (P("grp", None), P(), P(None, "grp", "dom"), P(), P(), P(), P(), P())
    return jax.shard_map(
        per_device, mesh=mesh, in_specs=in_specs, out_specs=out_specs, check_vma=False
    )
```

profile of v0, /device:TPU:0, one launch (start us, length us, event | category | flops | bytes accessed | tf_op | source)
XLA Modules:
  0.0 2275.9 jit_solution(12449745818382014852)
XLA Ops:
  7.7 5.1 collective-permute-start
  17.3 164.5 %gather_fusion.1 = f32[49152,4]{1,0:T(8,128)} fusion(f32[4,3072]{0,1:T(8,128)} %copy.220, s32[49152]{0:T(1024)S(1)} %broadcast_clamp_fusion), kind=kCustom, calls=%fused_computation.1 | custom fusion | bytes 1769472 | tf_op jit(solution)/shard_map/jvp()/gather | solution.py:197
  181.7 17.6 multiply_bitcast_fusion.1
  199.3 15.5 copy.221
  216.5 164.5 %gather_fusion = f32[49152,3]{1,0:T(8,128)} fusion(f32[3,3072]{0,1:T(8,128)} %copy.218, s32[49152]{0:T(1024)S(1)} %broadcast_clamp_fusion), kind=kCustom, calls=%fused_computation | custom fusion | bytes 1376256 | tf_op jit(solution)/shard_map/jvp()/gather | solution.py:197
  381.0 15.3 copy.272
  435.7 6.1 fusion.24
  441.9 7.9 bitcast_multiply_fusion
  450.9 20.8 copy.224
  471.7 4.1 broadcast_multiply_fusion.1
  475.8 14.3 copy.225
  490.2 40.7 %convert_bitcast_fusion.1 = bf16[40,49,1024]{1,0,2:T(8,128)(2,1)} fusion(f32[49,48,1024]{0,1,2:T(8,128)} %copy.224, f32[40,48,1024]{1,0,2:T(8,128)} %copy.225), kind=kOutput, calls=%fused_computation.11 | convolution fusion | flops 1158062080 | bytes 21512192 | tf_op jit(solution)/shard_map/jvp(mka,lka->mla)/dot_general | solution.py:106
  530.9 13.9 reshape.414
  544.8 12.8 fusion.28
  567.4 4.3 collective-permute-start.4
  571.7 9.0 scatter_custom_fusion.1
  580.6 4.4 copy.230
  586.7 164.7 %gather_fusion.2 = f32[49152,4]{1,0:T(8,128)} fusion(f32[4,3072]{0,1:T(8,128)} %copy.227, s32[49152]{0:T(1024)S(1)} %broadcast_clamp_fusion), kind=kCustom, calls=%fused_computation.2 | custom fusion | bytes 1769472 | tf_op jit(solution)/shard_map/jvp()/gather | solution.py:197
  751.4 17.6 multiply_bitcast_fusion
  769.0 14.8 copy.228
  783.8 6.1 broadcast_multiply_fusion
  789.9 14.3 copy.232
  804.1 40.8 %convert_bitcast_fusion = bf16[40,49,1024]{1,0,2:T(8,128)(2,1)} fusion(f32[49,48,1024]{0,1,2:T(8,128)} %copy.224, f32[40,48,1024]{1,0,2:T(8,128)} %copy.232), kind=kOutput, calls=%fused_computation.10 | convolution fusion | flops 1158062080 | bytes 21512192 | tf_op jit(solution)/shard_map/jvp(mka,lka->mla)/dot_general | solution.py:106
  844.9 13.9 reshape.415
  858.8 12.7 fusion.31
  871.6 4.1 fusion.62
  875.7 7.7 scatter_custom_fusion
  883.5 63.0 %all-reduce.9 = (f32[512,4]{1,0:T(8,128)S(1)}, f32[512]{0:T(512)}) all-reduce(f32[512,4]{1,0:T(8,128)S(1)} %copy-done.53, f32[512]{0:T(512)S(1)} %scatter_custom_fusion), channel_id=1, replica_groups=mesh['dom'=16,'grp'=2] {'dom'}, use_global_device_ids=true, to_apply=%region_7.8 | all-reduce | flops 2560 | bytes 20480 | tf_op jit(solution)/shard_map/psum | solution.py:218
  949.4 4.9 all-reduce.10
  966.6 14.2 convolution_bitcast_fusion.3
  980.9 8.6 reshape.319
  989.5 15.0 copy.235
  1004.5 47.5 %fusion.412 = f32[1024,49,48]{1,2,0:T(8,128)} fusion(f32[1024,49,40]{1,2,0:T(8,128)} %copy.235, f32[40,48,1024]{1,0,2:T(8,128)} %copy.232), kind=kOutput, calls=%fused_computation.696 | convolution fusion | flops 1156055040 | bytes 25526272 | tf_op jit(solution)/shard_map/transpose(jvp(mka,lka->mla))/dot_general | solution.py:106
  1052.0 45.6 %convolution_bitcast_fusion.1 = f32[40,48,1024]{1,0,2:T(8,128)} fusion(f32[1024,49,40]{1,2,0:T(8,128)S(1)} %copy-done.5, f32[49,48,1024]{0,1,2:T(8,128)} %copy.224), kind=kOutput, calls=%fused_computation.13 | convolution fusion | flops 1156055040 | bytes 25526272 | tf_op jit(solution)/shard_map/transpose(jvp(mka,lka->mla))/dot_general | solution.py:106
  1097.6 15.2 copy.237
  1112.8 6.6 multiply_reduce_fusion
  1119.4 6.7 fusion.52
  1126.1 6.7 fusion.27
  1132.8 19.2 copy.258
  1152.1 5.7 fusion.93
  1157.9 6.3 multiply_add_fusion.22
  1182.7 5.0 fusion.35
  1188.7 13.8 copy.275
  1202.5 262.0 %scatter_custom_fusion.2 = f32[4,3072]{0,1:T(8,128)} fusion(s32[49152]{0:T(1024)} %bitcast.687, f32[49152,4]{1,0:T(8,128)} %bitcast.683, f32[]{:T(128)} %constant.254.clone.1), kind=kCustom, calls=%fused_computation.113 | custom fusion | flops 196608 | bytes 49664 | tf_op jit(solution)/shard_map/transpose(jvp())/scatter-add | solution.py:197
  1472.1 3.6 collective-permute-start.6
  1480.0 4.7 copy.322
  1487.9 7.0 fusion.58
  1495.0 12.9 convolution_bitcast_fusion.2
  1507.9 8.6 reshape.321
  1516.5 15.0 copy.243
  1531.5 46.1 %convolution_bitcast_fusion = f32[40,48,1024]{1,0,2:T(8,128)} fusion(f32[1024,49,40]{1,2,0:T(8,128)} %copy.243, f32[49,48,1024]{0,1,2:T(8,128)} %copy.224), kind=kOutput, calls=%fused_computation.12 | convolution fusion | flops 1156055040 | bytes 25526272 | tf_op jit(solution)/shard_map/transpose(jvp(mka,lka->mla))/dot_general | solution.py:106
  1577.6 46.5 %fusion.411 = f32[1024,49,48]{1,2,0:T(8,128)} fusion(f32[1024,49,40]{1,2,0:T(8,128)S(1)} %copy-done.4, f32[40,48,1024]{1,0,2:T(8,128)} %copy.225), kind=kOutput, calls=%fused_computation.695 | convolution fusion | flops 1156055040 | bytes 25526272 | tf_op jit(solution)/shard_map/transpose(jvp(mka,lka->mla))/dot_general | solution.py:106
  1624.1 15.3 copy.248
  1639.4 4.9 multiply_reduce_fusion.1
  1646.8 6.6 fusion.49
  1653.4 7.0 fusion.26
  1660.4 18.8 copy.245
  1679.3 4.8 fusion.83
  1684.1 5.1 multiply_add_fusion.23
  1699.1 12.7 copy.279
  1711.9 12.7 copy.277
  1724.5 261.7 %scatter_fusion.1 = f32[3,3072]{0,1:T(8,128)S(1)} fusion(f32[3,3072]{0,1:T(8,128)S(1)} %pad.31.clone, s32[49152]{0:T(1024)S(1)} %bitcast.688, f32[49152,3]{1,0:T(8,128)} %bitcast.681), kind=kCustom, calls=%fused_computation.7 | custom fusion | flops 147456 | bytes 1966080 | tf_op jit(solution)/shard_map/transpose(jvp())/scatter-add | solution.py:197
  1987.4 237.1 %scatter_fusion = f32[3,3072]{0,1:T(8,128)} fusion(f32[3,3072]{0,1:T(8,128)} %pad.27.clone, s32[49152]{0:T(1024)S(1)} %bitcast.689, f32[49152,3]{1,0:T(8,128)} %bitcast.680), kind=kCustom, calls=%fused_computation.6 | custom fusion | flops 147456 | bytes 1966080 | tf_op jit(solution)/shard_map/transpose(jvp())/scatter-add | solution.py:197
  2233.2 40.4 %all-reduce.8 = (f32[10,12]{1,0:T(8,128)}, f32[4,512]{1,0:T(4,128)}, f32[512,4]{0,1:T(4,128)}, f32[10,12]{1,0:T(8,128)}, f32[4,512]{1,0:T(4,128)}) all-reduce(f32[10,12]{1,0:T(8,128)S(1)} %copy-done.75, f32[4,512]{1,0:T(4,128)S(1)} %copy-done.72, f32[512,4]{0,1:T(4,128)S(1)} %fusion.359, ...), channel_id=1, replica_groups=mesh['dom'=16,'grp'=2] {'dom','grp'}, use_global_device_ids=true, to_apply=%region_24.25 | all-reduce | flops 6384 | bytes 51072 | tf_op jit(solution)/shard_map/psum | solution.py:241
  (314 shorter events, 120.5 us)
Async XLA Ops:
  0.6 870.9 %copy-start = (f32[4,512]{1,0:T(4,128)S(1)}, f32[4,512]{1,0:T(4,128)}, u32[]{:S(2)}) copy-start(f32[4,512]{1,0:T(4,128)} %param.25) | copy-start | bytes 24580
  1.3 14.1 collective-permute-start.3
  2.6 12.9 collective-permute-start.2
  6.4 393.0 %copy-start.57 = (f32[3,1,1024]{2,0,1:T(4,128)}, f32[3,1,1024]{2,0,1:T(4,128)S(1)}, u32[]{:S(2)}) copy-start(f32[3,1,1024]{2,0,1:T(4,128)S(1)} %copy.324) | copy-start | bytes 36868
  6.4 208.5 %collective-permute-start.1 = (f32[3,1024]{1,0:T(4,128)S(1)}, f32[3,1024]{1,0:T(4,128)S(1)}, u32[]{:S(2)}, u32[]{:S(2)}) collective-permute-start(f32[3,1024]{1,0:T(4,128)S(1)} %bitcast.692), channel_id=1, source_target_pairs={{2,0},{4,2},{6,4},{8,6},{10,8},{12,10},{14,12},{16,14},{18,16},{20... | collective-permute-start | bytes 36872 | tf_op jit(solution)/shard_map/ppermute | solution.py:32
  7.7 207.2 %collective-permute-start = (f32[3,1024]{1,0:T(4,128)S(1)}, f32[3,1024]{1,0:T(4,128)S(1)}, u32[]{:S(2)}, u32[]{:S(2)}) collective-permute-start(f32[3,1024]{1,0:T(4,128)S(1)} %bitcast.693), channel_id=1, source_target_pairs={{0,2},{2,4},{4,6},{6,8},{8,10},{10,12},{12,14},{14,16},{16,18},{18... | collective-permute-start | bytes 36872 | tf_op jit(solution)/shard_map/ppermute | solution.py:30
  14.7 184.7 %copy-start.45 = (s32[48,1024,1]{1,2,0:T(1,128)}, s32[48,1024,1]{1,2,0:T(1,128)S(1)}, u32[]{:S(2)}) copy-start(s32[48,1024,1]{1,2,0:T(1,128)S(1)} %compare_select_fusion) | copy-start | bytes 589828
  15.5 735.9 %copy-start.42 = (f32[48,1024]{1,0:T(8,128)}, f32[48,1024]{1,0:T(8,128)S(1)}, u32[]{:S(2)}) copy-start(f32[48,1024]{1,0:T(8,128)S(1)} %fusion.340) | copy-start | bytes 589828
  396.3 12.9 copy-start.31
  397.8 44.1 %copy-start.35 = (f32[48,1024]{1,0:T(8,128)}, f32[48,1024]{1,0:T(8,128)S(1)}, u32[]{:S(2)}) copy-start(f32[48,1024]{1,0:T(8,128)S(1)} %get-tuple-element.132) | copy-start | bytes 589828
  399.4 42.5 %copy-start.10 = (f32[12,48,1024]{2,1,0:T(8,128)}, f32[12,48,1024]{2,1,0:T(8,128)S(1)}, u32[]{:S(2)}) copy-start(f32[12,48,1024]{2,1,0:T(8,128)S(1)} %subtract_dynamic-update-slice_fusion) | copy-start | bytes 7077892
  399.5 35.4 %copy-start.2 = (f32[3,48,1024]{2,1,0:T(8,128)}, f32[3,48,1024]{2,1,0:T(8,128)S(1)}, u32[]{:S(2)}) copy-start(f32[3,48,1024]{2,1,0:T(8,128)S(1)} %fusion.70) | copy-start | bytes 1769476
  400.4 29.0 %copy-start.18 = (f32[1,48,1024]{2,1,0:T(8,128)}, f32[1,48,1024]{2,1,0:T(8,128)S(1)}, u32[]{:S(2)}) copy-start(f32[1,48,1024]{2,1,0:T(8,128)S(1)} %get-tuple-element.113) | copy-start | bytes 589828
  401.9 29.2 %copy-start.20 = (f32[1,48,1024]{2,1,0:T(8,128)}, f32[1,48,1024]{2,1,0:T(8,128)S(1)}, u32[]{:S(2)}) copy-start(f32[1,48,1024]{2,1,0:T(8,128)S(1)} %get-tuple-element.111) | copy-start | bytes 589828
  402.6 25.9 %copy-start.23 = (f32[1,48,1024]{2,1,0:T(8,128)}, f32[1,48,1024]{2,1,0:T(8,128)S(1)}, u32[]{:S(2)}) copy-start(f32[1,48,1024]{2,1,0:T(8,128)S(1)} %get-tuple-element.109) | copy-start | bytes 589828
  405.5 26.3 %copy-start.26 = (f32[1,48,1024]{2,1,0:T(8,128)}, f32[1,48,1024]{2,1,0:T(8,128)S(1)}, u32[]{:S(2)}) copy-start(f32[1,48,1024]{2,1,0:T(8,128)S(1)} %get-tuple-element.107) | copy-start | bytes 589828
  406.3 28.7 %copy-start.6 = (f32[1,48,1024]{2,1,0:T(8,128)}, f32[1,48,1024]{2,1,0:T(8,128)S(1)}, u32[]{:S(2)}) copy-start(f32[1,48,1024]{2,1,0:T(8,128)S(1)} %get-tuple-element.105) | copy-start | bytes 589828
  410.6 24.3 %copy-start.8 = (f32[1,48,1024]{2,1,0:T(8,128)}, f32[1,48,1024]{2,1,0:T(8,128)S(1)}, u32[]{:S(2)}) copy-start(f32[1,48,1024]{2,1,0:T(8,128)S(1)} %get-tuple-element.103) | copy-start | bytes 589828
  419.4 16.3 copy-start.70
  426.3 15.6 copy-start.67
  450.9 20.8 copy-start.40
  544.8 16.1 copy-start.62
  544.8 16.1 copy-start.76
  544.8 19.5 copy-start.69
  563.7 384.0 %copy-start.13 = (f32[512,1024]{1,0:T(8,128)}, f32[512,1024]{1,0:T(8,128)S(1)}, u32[]{:S(2)}) copy-start(f32[512,1024]{1,0:T(8,128)S(1)} %get-tuple-element.101) | copy-start | bytes 6291460
  564.3 187.1 %copy-start.63 = (f32[1024]{0:T(1024)}, f32[1024]{0:T(1024)S(1)}, u32[]{:S(2)}) copy-start(f32[1024]{0:T(1024)S(1)} %fusion.372) | copy-start | bytes 12292
  566.1 18.9 collective-permute-start.5
  567.4 17.6 collective-permute-start.4
  783.8 20.4 copy-start.38
  871.6 11.9 copy-start.53
  871.6 75.7 %copy-start.83 = (f32[1,512]{1,0:T(1,128)S(1)}, f32[1,512]{1,0:T(1,128)}, u32[]{:S(2)}) copy-start(f32[1,512]{1,0:T(1,128)} %param.18) | copy-start | bytes 6148
  946.4 34.4 %copy-start.59 = (f32[512,4]{1,0:T(8,128)}, f32[512,4]{1,0:T(8,128)S(1)}, u32[]{:S(2)}) copy-start(f32[512,4]{1,0:T(8,128)S(1)} %get-tuple-element.67) | copy-start | bytes 24580
  1004.5 47.5 %copy-start.5 = (f32[1024,49,40]{1,2,0:T(8,128)S(1)}, f32[1024,49,40]{1,2,0:T(8,128)}, u32[]{:S(2)}) copy-start(f32[1024,49,40]{1,2,0:T(8,128)} %copy.235) | copy-start | bytes 24084484
  1097.6 15.2 copy-start.39
  1112.8 13.3 copy-start.68
  1132.8 19.3 copy-start.3
  1132.8 19.3 copy-start.7
  1132.8 19.3 copy-start.9
  1132.8 19.3 copy-start.19
  1157.9 19.5 copy-start.79
  1177.3 10.4 copy-start.43
  1177.3 10.4 copy-start.44
  1177.4 25.1 %copy-start.82 = (f32[4]{0:T(128)}, f32[4]{0:T(128)S(1)}, u32[]{:S(2)}) copy-start(f32[4]{0:T(128)S(1)} %pad_maximum_fusion.3) | copy-start | bytes 52
  1202.5 276.2 %copy-start.81 = (f32[512]{0:T(512)S(1)}, f32[512]{0:T(512)}, u32[]{:S(2)}) copy-start(f32[512]{0:T(512)} %get-tuple-element.68) | copy-start | bytes 6148
  1202.5 284.8 %copy-start.66 = (f32[1024]{0:T(1024)S(1)}, f32[1024]{0:T(1024)}, u32[]{:S(2)}) copy-start(f32[1024]{0:T(1024)} %copy-done.65) | copy-start | bytes 12292
  1202.5 285.4 %copy-start.64 = (f32[1024]{0:T(1024)S(1)}, f32[1024]{0:T(1024)}, u32[]{:S(2)}) copy-start(f32[1024]{0:T(1024)} %copy-done.63) | copy-start | bytes 12292
  1470.8 15.7 collective-permute-start.7
  1472.1 14.4 collective-permute-start.6
  1531.5 46.1 %copy-start.4 = (f32[1024,49,40]{1,2,0:T(8,128)S(1)}, f32[1024,49,40]{1,2,0:T(8,128)}, u32[]{:S(2)}) copy-start(f32[1024,49,40]{1,2,0:T(8,128)} %copy.243) | copy-start | bytes 24084484
  1644.4 9.1 copy-start.71
  1660.4 18.8 copy-start.22
  1660.4 18.8 copy-start.25
  1660.4 18.8 copy-start.28
  1684.1 8.0 copy-start.32
  1711.9 12.7 copy-start.46
  1987.4 243.9 %copy-start.14 = (f32[512,1024]{1,0:T(8,128)S(1)}, f32[512,1024]{1,0:T(8,128)}, u32[]{:S(2)}) copy-start(f32[512,1024]{1,0:T(8,128)} %copy-done.13) | copy-start | bytes 6291460
  1987.4 243.9 %copy-start.61 = (f32[4,1024]{1,0:T(4,128)S(1)}, f32[4,1024]{1,0:T(4,128)}, u32[]{:S(2)}) copy-start(f32[4,1024]{1,0:T(4,128)} %copy-done.60) | copy-start | bytes 49156
  1987.4 245.7 %copy-start.72 = (f32[4,512]{1,0:T(4,128)S(1)}, f32[4,512]{1,0:T(4,128)}, u32[]{:S(2)}) copy-start(f32[4,512]{1,0:T(4,128)} %fusion.356) | copy-start | bytes 24580
  1987.4 245.7 %copy-start.73 = (f32[10,12]{1,0:T(8,128)S(1)}, f32[10,12]{1,0:T(8,128)}, u32[]{:S(2)}) copy-start(f32[10,12]{1,0:T(8,128)} %fusion.52) | copy-start | bytes 1444
  1987.4 245.7 %copy-start.74 = (f32[4,512]{1,0:T(4,128)S(1)}, f32[4,512]{1,0:T(4,128)}, u32[]{:S(2)}) copy-start(f32[4,512]{1,0:T(4,128)} %fusion.355) | copy-start | bytes 24580
  1987.4 245.7 %copy-start.75 = (f32[10,12]{1,0:T(8,128)S(1)}, f32[10,12]{1,0:T(8,128)}, u32[]{:S(2)}) copy-start(f32[10,12]{1,0:T(8,128)} %fusion.49) | copy-start | bytes 1444
  1987.4 288.3 %copy-start.1 = (f32[4,512]{1,0:T(4,128)S(1)}, f32[4,512]{1,0:T(4,128)}, u32[]{:S(2)}) copy-start(f32[4,512]{1,0:T(4,128)} %param.25) | copy-start | bytes 24580
  2228.6 45.0 %collective-permute-start.8 = (f32[3,1024]{0,1:T(8,128)}, f32[3,1024]{0,1:T(8,128)S(1)}, u32[]{:S(2)}, u32[]{:S(2)}) collective-permute-start(f32[3,1024]{0,1:T(8,128)} %get-tuple-element.124), channel_id=1, source_target_pairs={{0,2},{2,4},{4,6},{6,8},{8,10},{10,12},{12,14},{14,16},{16,18},{18... | collective-permute-start | bytes 36872 | tf_op jit(solution)/shard_map/ppermute | solution.py:30
  2229.9 43.6 %collective-permute-start.9 = (f32[3,1024]{0,1:T(8,128)S(1)}, f32[3,1024]{0,1:T(8,128)}, u32[]{:S(2)}, u32[]{:S(2)}) collective-permute-start(f32[3,1024]{0,1:T(8,128)S(1)} %get-tuple-element.125), channel_id=1, source_target_pairs={{2,0},{4,2},{6,4},{8,6},{10,8},{12,10},{14,12},{16,14},{18,16},{20... | collective-permute-start | bytes 36872 | tf_op jit(solution)/shard_map/ppermute | solution.py:32
  (30 other events, 155.8 us)
where the time goes:
time: 2280 us
  other arithmetic  922 us (40%)
  local copies, waits for them, and re-layouts  815 us (36%)
  matrix products  386 us (17%)
  blocking collectives  108 us (5%)
  starting transfers between devices  23.8 us (1%)
    scatter-add x2, other arithmetic, layer_density(): sites_all[:, slot_index]  499 us
    gather x2, local copies, waits for them, and re-layouts, layer_density(): weights_all[:, slot_index]  329 us
    dot_general x6, matrix products, densities(): jnp.einsum('mka,lka->mla', mixed_terms, angular, precision=highest)  267 us
    scatter-add x1, other arithmetic, layer_density(): weights_all[:, slot_index]  262 us
    gather x2, local copies, waits for them, and re-layouts, layer_density(): sites_all[:, slot_index]  180 us
    psum x1, blocking collectives, per_device(): energy_sum, species_count = lax.psum((energy_part, count_part), 'dom')  63 us
    transpose x4, local copies, waits for them, and re-layouts, densities(): jnp.einsum('mka,lka->mla', mixed_terms, angular, precision=highest)  60.5 us
  transfers between devices with their start and end apart: 10, of which 0 were waited for; matrix products, arithmetic and copies ran while one was open for 10% of the time, Pallas kernels for 0%

commit v1 on v0

v1 whole, which is shorter than its diff:
```python
from functools import partial, reduce
import math

import jax
import jax.numpy as jnp
from jax import lax
from jax.experimental import pallas as pl
from jax.experimental.pallas import tpu as pltpu
from jax.sharding import PartitionSpec as P

NRAD = 12
NMAX = 10
LMAX = 6
LM = 49
SPECIES = 4
CH = SPECIES * NMAX
DENS = CH * LM
NBR = 48
NPAD = 64
TILE = 128
LBLK = 7
WROWS = 4
NVAL = 7

cutoff_radius = 5.0
density_scale = 0.17
norm_eps = 1e-05
ridge_weight = 0.1
highest = lax.Precision.HIGHEST
f32 = jnp.float32
bf16 = jnp.bfloat16


def shift_pair(cells, axis):
    count = lax.axis_size(axis)
    ends = count - 1
    left = lax.ppermute(cells, axis, [(i, i + 1) for i in range(ends)])
    right = lax.ppermute(cells, axis, [(i + 1, i) for i in range(ends)])
    return left, right


def double_factorial(number):
    result = 1.0
    while number > 1:
        result = result * number
        number = number - 2
    return result


def norm_of(degree, azimuth):
    value = math.sqrt(
        (2 * degree + 1)
        / (4 * math.pi)
        * math.factorial(degree - azimuth)
        / math.factorial(degree + azimuth)
    )
    return value * (math.sqrt(2.0) if azimuth else 1.0)


def scaled_legendre(coord_z):
    table = {}
    for azimuth in range(LMAX + 1):
        table[azimuth, azimuth] = norm_of(azimuth, azimuth) * double_factorial(2 * azimuth - 1)
        if azimuth + 1 <= LMAX:
            ratio = norm_of(azimuth + 1, azimuth) / norm_of(azimuth, azimuth)
            table[azimuth + 1, azimuth] = coord_z * (
                (2 * azimuth + 1) * ratio * table[azimuth, azimuth]
            )
        for degree in range(azimuth + 2, LMAX + 1):
            gap = degree - azimuth
            first = (2 * degree - 1) / gap * norm_of(degree, azimuth) / norm_of(degree - 1, azimuth)
            second = (
                (degree + azimuth - 1) / gap * norm_of(degree, azimuth) / norm_of(degree - 2, azimuth)
            )
            table[degree, azimuth] = (first * coord_z) * table[degree - 1, azimuth] - (
                second * table[degree - 2, azimuth]
            )
    return table


def azimuth_powers(coord_x, coord_y):
    cosines = [None, coord_x]
    sines = [None, coord_y]
    for _ in range(2, LMAX + 1):
        cosines.append(cosines[-1] * coord_x - sines[-1] * coord_y)
        sines.append(sines[-1] * coord_x + cosines[-2] * coord_y)
    return cosines, sines


def fetch(tab_ref, names, hi, lo, row_low, row_high):
    def body(row, values):
        hit = hi == row
        out = []
        for name, value in zip(names, values):
            line = jnp.broadcast_to(tab_ref[pl.ds(name * 24 + row, 1), :], (8, TILE))
            got = jnp.take_along_axis(line, lo, axis=1, mode="promise_in_bounds")
            out.append(jnp.where(hit, got, value))
        return tuple(out)

    zero = jnp.zeros((8, TILE), f32)
    return lax.fori_loop(row_low, row_high + 1, body, tuple(zero for _ in names))


def edge_block(layer, tab_ref, cen_ref, idx_ref, wt_ref, block_at, row_low, row_high):
    base = pl.multiple_of(block_at * 8, 8)
    index = idx_ref[pl.ds(base, 8), :]
    weight = wt_ref[pl.ds(base, 8), :]
    hi = lax.shift_right_logical(index, 7)
    lo = lax.bitwise_and(index, 127)
    names = (0, 1, 2, 3) if layer == 1 else (0, 1, 2, 3, 4, 5, 6)
    values = fetch(tab_ref, names, hi, lo, row_low, row_high)
    live = weight > 0.0
    deltas = []
    for axis in range(3):
        centre = jnp.broadcast_to(cen_ref[pl.ds(axis, 1), :], (8, TILE))
        deltas.append(jnp.where(live, values[axis] - centre, 1.0))
    dist = jnp.sqrt(deltas[0] * deltas[0] + deltas[1] * deltas[1] + deltas[2] * deltas[2])
    inv = 1.0 / dist
    unit = [delta * inv for delta in deltas]
    if layer == 1:
        chan = [jnp.where(values[3] == float(c), 1.0, 0.0) for c in range(SPECIES)]
    else:
        chan = list(values[3:])
    return hi, lo, weight, dist, inv, unit, chan


def radial_terms(dist, rad_ref, with_slope):
    scaled = dist * (2.0 / cutoff_radius) - 1.0
    inside = dist < cutoff_radius
    angle = dist * (math.pi / cutoff_radius)
    cutoff = jnp.where(inside, 0.5 * (jnp.cos(angle) + 1.0), 0.0)
    cheb = [None, scaled]
    twice = 2.0 * scaled
    cheb.append(twice * scaled - 1.0)
    for _ in range(3, NRAD):
        cheb.append(twice * cheb[-1] - cheb[-2])
    basis = [cutoff] + [cutoff * cheb[p] for p in range(1, NRAD)]
    radial = []
    for n in range(NMAX):
        total = basis[0] * rad_ref[n, 0]
        for p in range(1, NRAD):
            total = total + basis[p] * rad_ref[n, p]
        radial.append(total)
    if not with_slope:
        return basis, radial, None
    slope_cut = jnp.where(inside, (-0.5 * math.pi / cutoff_radius) * jnp.sin(angle), 0.0)
    grad_scaled = cutoff * (2.0 / cutoff_radius)
    second = [None, None, twice]
    second[1] = jnp.ones_like(scaled)
    for _ in range(3, NRAD):
        second.append(twice * second[-1] - second[-2])
    slopes = [slope_cut, slope_cut * scaled + grad_scaled]
    for p in range(2, NRAD):
        slopes.append(slope_cut * cheb[p] + grad_scaled * (float(p) * second[p]))
    return basis, radial, slopes


def harmonic_list(unit):
    table = scaled_legendre(unit[2])
    cosines, sines = azimuth_powers(unit[0], unit[1])
    columns = []
    for degree in range(LMAX + 1):
        for signed in range(-degree, degree + 1):
            azimuth = abs(signed)
            poly = table[degree, azimuth]
            if signed == 0:
                columns.append(poly)
            elif signed > 0:
                columns.append(poly * cosines[azimuth])
            else:
                columns.append(poly * sines[azimuth])
    columns[0] = jnp.full_like(unit[2], columns[0])
    return columns


def density_kernel(layer, cnt_ref, row_ref, rad_ref, tab_ref, cen_ref, idx_ref, wt_ref, out_ref,
                   x_ref, y_ref, d_ref):
    tile = pl.program_id(0)
    count = cnt_ref[tile]
    row_low, row_high = row_ref[0, tile], row_ref[1, tile]
    blocks = lax.div(count + 7, 8)

    def edges(block_at, carry):
        base = pl.multiple_of(block_at * 8, 8)
        hi, lo, weight, dist, inv, unit, chan = edge_block(
            layer, tab_ref, cen_ref, idx_ref, wt_ref, block_at, row_low, row_high
        )
        _, radial, _ = radial_terms(dist, rad_ref, False)
        for c in range(SPECIES):
            scale = chan[c] * weight
            for n in range(NMAX):
                x_ref[pl.ds(base * CH + (c * NMAX + n), 8, stride=CH), :] = scale * radial[n]
        for at, column in enumerate(harmonic_list(unit)):
            y_ref[pl.ds(at * NPAD + base, 8), :] = column
        return carry

    lax.fori_loop(0, blocks, edges, 0)
    pairs = lax.div(count + 1, 2)

    def lm_block(block_at, carry):
        first = block_at * LBLK

        def slots(pair, acc):
            acc = list(acc)
            for part in range(2):
                slot = pair * 2 + part
                rows = [
                    x_ref[pl.ds(pl.multiple_of(slot * CH + 8 * j, 8), 8), :] for j in range(CH // 8)
                ]
                for at in range(LBLK):
                    line = jnp.broadcast_to(
                        y_ref[pl.ds((first + at) * NPAD + slot, 1), :], (8, TILE)
                    )
                    for j in range(CH // 8):
                        acc[at * (CH // 8) + j] = acc[at * (CH // 8) + j] + rows[j] * line
            return tuple(acc)

        zero = jnp.zeros((8, TILE), f32)
        acc = lax.fori_loop(0, pairs, slots, tuple(zero for _ in range(LBLK * (CH // 8))))
        for at in range(LBLK):
            for j in range(CH // 8):
                d_ref[pl.ds(8 * j * LM + first + at, 8, stride=LM), :] = acc[at * (CH // 8) + j]
        return carry

    lax.fori_loop(0, LM // LBLK, lm_block, 0)
    out_ref[...] = d_ref[...].astype(bf16)


def smem_spec():
    return pl.BlockSpec(memory_space=pltpu.SMEM)


def tile_spec(rows):
    return pl.BlockSpec((rows, TILE), lambda i: (0, i))


def whole_spec(shape):
    return pl.BlockSpec(shape, lambda i: tuple(0 for _ in shape))


def density_call(layer, counts, rows, radial, table, centres, index, weight):
    atoms = centres.shape[1]
    return pl.pallas_call(
        partial(density_kernel, layer),
        out_shape=jax.ShapeDtypeStruct((DENS, atoms), bf16),
        grid=(atoms // TILE,),
        in_specs=[
            smem_spec(),
            smem_spec(),
            smem_spec(),
            whole_spec(table.shape),
            tile_spec(8),
            tile_spec(NPAD),
            tile_spec(NPAD),
        ],
        out_specs=tile_spec(DENS),
        scratch_shapes=[
            pltpu.VMEM((NPAD * CH, TILE), f32),
            pltpu.VMEM((LM * NPAD, TILE), f32),
            pltpu.VMEM((DENS, TILE), f32),
        ],
        compiler_params=pltpu.CompilerParams(vmem_limit_bytes=48 << 20),
        name="density_%d" % layer,
    )(counts, rows, radial, table, centres, index, weight)


def backward_kernel(layer, cnt_ref, row_ref, rad_ref, tab_ref, cen_ref, idx_ref, wt_ref, dd_ref,
                    win_ref, own_ref, rgr_ref, x_ref, y_ref, gx_ref, gy_ref, val_ref):
    tile = pl.program_id(0)
    count = cnt_ref[tile]
    row_low, row_high = row_ref[0, tile], row_ref[1, tile]
    blocks = lax.div(count + 7, 8)
    chunks = lax.div(count + 31, 32)

    @pl.when(tile == 0)
    def _():
        win_ref[...] = jnp.zeros_like(win_ref)
        rgr_ref[...] = jnp.zeros_like(rgr_ref)

    def edges(block_at, carry):
        base = pl.multiple_of(block_at * 8, 8)
        hi, lo, weight, dist, inv, unit, chan = edge_block(
            layer, tab_ref, cen_ref, idx_ref, wt_ref, block_at, row_low, row_high
        )
        _, radial, _ = radial_terms(dist, rad_ref, False)
        for c in range(SPECIES):
            scale = chan[c] * weight
            for n in range(NMAX):
                x_ref[pl.ds((c * NMAX + n) * NPAD + base, 8), :] = scale * radial[n]
        for at, column in enumerate(harmonic_list(unit)):
            y_ref[pl.ds(at * NPAD + base, 8), :] = column
        return carry

    lax.fori_loop(0, chunks * 4, edges, 0)

    zero = jnp.zeros((8, TILE), f32)

    def chunk_body(chunk, carry):
        start = pl.multiple_of(chunk * 32, 32)

        def m_block(block_at, inner):
            def over_lm(lm, acc):
                acc = list(acc)
                lines = [
                    jnp.broadcast_to(dd_ref[pl.ds((block_at * 8 + i) * LM + lm, 1), :], (8, TILE))
                    for i in range(8)
                ]
                for kb in range(4):
                    col = y_ref[pl.ds(pl.multiple_of(lm * NPAD + start + 8 * kb, 8), 8), :]
                    for i in range(8):
                        acc[i * 4 + kb] = acc[i * 4 + kb] + lines[i] * col
                return tuple(acc)

            acc = lax.fori_loop(0, LM, over_lm, tuple(zero for _ in range(32)))
            for i in range(8):
                for kb in range(4):
                    at = pl.multiple_of((block_at * 8 + i) * NPAD + start + 8 * kb, 8)
                    gx_ref[pl.ds(at, 8), :] = acc[i * 4 + kb]
            return inner

        lax.fori_loop(0, CH // 8, m_block, 0)

        def lm_block(block_at, inner):
            def over_m(m, acc):
                acc = list(acc)
                lines = [
                    jnp.broadcast_to(dd_ref[pl.ds(m * LM + block_at * LBLK + i, 1), :], (8, TILE))
                    for i in range(LBLK)
                ]
                for kb in range(4):
                    col = x_ref[pl.ds(pl.multiple_of(m * NPAD + start + 8 * kb, 8), 8), :]
                    for i in range(LBLK):
                        acc[i * 4 + kb] = acc[i * 4 + kb] + lines[i] * col
                return tuple(acc)

            acc = lax.fori_loop(0, CH, over_m, tuple(zero for _ in range(LBLK * 4)))
            for i in range(LBLK):
                for kb in range(4):
                    at = pl.multiple_of((block_at * LBLK + i) * NPAD + start + 8 * kb, 8)
                    gy_ref[pl.ds(at, 8), :] = acc[i * 4 + kb]
            return inner

        lax.fori_loop(0, LM // LBLK, lm_block, 0)
        return carry

    lax.fori_loop(0, chunks, chunk_body, 0)

    def finish(block_at, own):
        base = pl.multiple_of(block_at * 8, 8)
        hi, lo, weight, dist, inv, unit, chan = edge_block(
            layer, tab_ref, cen_ref, idx_ref, wt_ref, block_at, row_low, row_high
        )
        basis, radial, slopes = radial_terms(dist, rad_ref, True)
        feat_grads = []
        radial_grads = [None] * NMAX
        for c in range(SPECIES):
            total = None
            for n in range(NMAX):
                grad = gx_ref[pl.ds((c * NMAX + n) * NPAD + base, 8), :]
                term = grad * radial[n]
                total = term if total is None else total + term
                piece = grad * chan[c]
                radial_grads[n] = piece if c == 0 else radial_grads[n] + piece
            feat_grads.append(total * weight)
        grad_r = None
        radial_grads = [grad * weight for grad in radial_grads]
        for p in range(NRAD):
            total = None
            for n in range(NMAX):
                at = (n * NRAD + p) * 8
                rgr_ref[pl.ds(at, 8), :] = rgr_ref[pl.ds(at, 8), :] + radial_grads[n] * basis[p]
                term = radial_grads[n] * rad_ref[n, p]
                total = term if total is None else total + term
            term = total * slopes[p]
            grad_r = term if grad_r is None else grad_r + term
        table = scaled_legendre(unit[2])
        cosines, sines = azimuth_powers(unit[0], unit[1])
        grad_x = grad_y = grad_z = None

        def plus(total, term):
            return term if total is None else total + term

        for azimuth in range(LMAX + 1):
            grad_cos = grad_sin = None
            for degree in range(azimuth, LMAX + 1):
                at = degree * degree + degree
                up = gy_ref[pl.ds((at + azimuth) * NPAD + base, 8), :]
                poly = table[degree, azimuth]
                if azimuth:
                    down = gy_ref[pl.ds((at - azimuth) * NPAD + base, 8), :]
                    grad_cos = plus(grad_cos, up * poly)
                    grad_sin = plus(grad_sin, down * poly)
                if degree > azimuth:
                    ratio = norm_of(degree, azimuth) / norm_of(degree, azimuth + 1)
                    slope = ratio * table[degree, azimuth + 1]
                    if azimuth:
                        grad_z = plus(grad_z, slope * (up * cosines[azimuth] + down * sines[azimuth]))
                    else:
                        grad_z = plus(grad_z, slope * up)
            if azimuth == 1:
                grad_x, grad_y = grad_cos, grad_sin
            elif azimuth > 1:
                below_cos, below_sin = cosines[azimuth - 1], sines[azimuth - 1]
                grad_x = grad_x + float(azimuth) * (grad_cos * below_cos + grad_sin * below_sin)
                grad_y = grad_y + float(azimuth) * (grad_sin * below_cos - grad_cos * below_sin)
        dot_u = grad_x * unit[0] + grad_y * unit[1] + grad_z * unit[2]
        live = weight > 0.0
        out = []
        for axis, grad in enumerate((grad_x, grad_y, grad_z)):
            value = (grad - dot_u * unit[axis]) * inv + grad_r * unit[axis]
            out.append(jnp.where(live, value, 0.0))
        values = out + feat_grads
        for at, value in enumerate(values):
            val_ref[pl.ds(at * NPAD + base, 8), :] = value
        return tuple(total + value for total, value in zip(own, out))

    own = lax.fori_loop(0, blocks, finish, (zero, zero, zero))
    own_ref[...] = jnp.concatenate(
        [jnp.sum(total, axis=0, keepdims=True) for total in own] + [jnp.zeros((5, TILE), f32)], axis=0
    )

    used = 3 if layer == 1 else NVAL
    sub = lax.broadcasted_iota(jnp.int32, (TILE, TILE), 0)
    windows = lax.div(row_high - row_low + WROWS, WROWS)

    def window(window_at, carry):
        row_base = row_low + window_at * WROWS

        def slot_block(block_at, acc):
            base = pl.multiple_of(block_at * 8, 8)
            index = idx_ref[pl.ds(base, 8), :]
            hi = lax.shift_right_logical(index, 7)
            lo = lax.bitwise_and(index, 127)
            tops, lows = [], []
            for value_at in range(used):
                value = val_ref[pl.ds(value_at * NPAD + base, 8), :]
                for row in range(WROWS):
                    tops.append(jnp.where(hi == row_base + row, value, 0.0))
            stacked = jnp.stack(tops, axis=0)
            ones, left = [], []
            for part in range(8):
                line = jnp.broadcast_to(lo[part : part + 1, :], (TILE, TILE))
                ones.append(jnp.where(line == sub, 1.0, 0.0).astype(bf16))
                left.append(stacked[:, part, :])
            left = jnp.concatenate(left, axis=1)
            ones = jnp.concatenate(ones, axis=1)
            high = left.astype(bf16)
            rest = (left - high.astype(f32)).astype(bf16)
            dims = (((1,), (1,)), ((), ()))
            acc = acc + lax.dot_general(high, ones, dims, preferred_element_type=f32)
            return acc + lax.dot_general(rest, ones, dims, preferred_element_type=f32)

        acc = lax.fori_loop(0, blocks, slot_block, jnp.zeros((used * WROWS, TILE), f32))
        for value_at in range(used):
            at = value_at * 32 + row_base
            win_ref[pl.ds(at, WROWS), :] = (
                win_ref[pl.ds(at, WROWS), :] + acc[value_at * WROWS : (value_at + 1) * WROWS]
            )
        return carry

    lax.fori_loop(0, windows, window, 0)


def backward_call(layer, counts, rows, radial, table, centres, index, weight, grad_dens):
    atoms = centres.shape[1]
    return pl.pallas_call(
        partial(backward_kernel, layer),
        out_shape=(
            jax.ShapeDtypeStruct((NVAL * 32, TILE), f32),
            jax.ShapeDtypeStruct((8, atoms), f32),
            jax.ShapeDtypeStruct((NMAX * NRAD * 8, TILE), f32),
        ),
        grid=(atoms // TILE,),
        in_specs=[
            smem_spec(),
            smem_spec(),
            smem_spec(),
            whole_spec(table.shape),
            tile_spec(8),
            tile_spec(NPAD),
            tile_spec(NPAD),
            tile_spec(DENS),
        ],
        out_specs=(
            whole_spec((NVAL * 32, TILE)),
            tile_spec(8),
            whole_spec((NMAX * NRAD * 8, TILE)),
        ),
        scratch_shapes=[
            pltpu.VMEM((CH * NPAD, TILE), f32),
            pltpu.VMEM((LM * NPAD, TILE), f32),
            pltpu.VMEM((CH * NPAD, TILE), f32),
            pltpu.VMEM((LM * NPAD, TILE), f32),
            pltpu.VMEM((NVAL * NPAD, TILE), f32),
        ],
        compiler_params=pltpu.CompilerParams(vmem_limit_bytes=48 << 20),
        name="backward_%d" % layer,
    )(counts, rows, radial, table, centres, index, weight, grad_dens)


def feature_map(invariants, mixing):
    inverse_rms = lax.rsqrt(jnp.mean(invariants * invariants, axis=0) + norm_eps)
    return jnp.einsum("qk,qa->ka", mixing, invariants, precision=highest) * inverse_rms


def small_solve(matrix, vector):
    order_n = matrix.shape[0]
    rows_now = [matrix[row_at] for row_at in range(order_n)]
    rights_now = [vector[row_at] for row_at in range(order_n)]
    for pivot_at in range(order_n):
        for below_at in range(pivot_at + 1, order_n):
            ratio_now = rows_now[below_at][pivot_at] / rows_now[pivot_at][pivot_at]
            rows_now[below_at] = rows_now[below_at] - ratio_now * rows_now[pivot_at]
            rights_now[below_at] = rights_now[below_at] - ratio_now * rights_now[pivot_at]
    answer = [None] * order_n
    for row_at in range(order_n - 1, -1, -1):
        running = rights_now[row_at]
        for later_at in range(row_at + 1, order_n):
            running = running - rows_now[row_at][later_at] * answer[later_at]
        answer[row_at] = running / rows_now[row_at][row_at]
    return jnp.stack(answer)


def contract(dens_in, coupling):
    factors = jnp.einsum("vdq,da->vqa", coupling, dens_in, preferred_element_type=f32)
    product = reduce(
        lambda earlier, later: earlier * later,
        [factors[index_v] for index_v in range(factors.shape[0])],
    )
    return (factors, product)


def contract_back(factors, upstream, coupling):
    partials = []
    for factor_at in range(factors.shape[0]):
        others = upstream
        for partner in range(factors.shape[0]):
            if partner != factor_at:
                others = others * factors[partner]
        partials.append(others)
    rounded = jnp.stack(partials).astype(bf16)
    return jnp.einsum("vdq,vqa->da", coupling, rounded, preferred_element_type=f32)


def as_rows(values, atoms):
    return values.reshape(values.shape[0] * (atoms // TILE), TILE)


def per_device(
    positions,
    species,
    neighbours,
    slot_counts,
    structure,
    target_energy,
    radial_one,
    coupling_one,
    coefficient_one,
    mixing,
    radial_two,
    coupling_two,
    coefficient_two,
):
    atoms = positions.shape[2]
    tiles = atoms // TILE
    centres = positions[:, 0, :]
    own_species = species[0]
    onehot = (own_species[None, :] == jnp.arange(SPECIES, dtype=jnp.int32)[:, None]).astype(f32)
    site = jnp.concatenate([centres, own_species.astype(f32)[None, :]], axis=0)
    site_left, site_right = shift_pair(site, "dom")
    site_ext = jnp.stack([site_left, site, site_right], axis=1)
    table_one = site_ext.reshape(4 * 3 * tiles, TILE)

    index = neighbours[:, 0, :] - (lax.axis_index("dom") - 1) * atoms
    live = jnp.arange(NBR, dtype=jnp.int32)[:, None] < slot_counts[0][None, :]
    own_row = jnp.broadcast_to(
        (jnp.arange(atoms, dtype=jnp.int32) // TILE + tiles)[None, :], (NBR, atoms)
    )
    block_row = jnp.where(live, index // TILE, own_row)
    counts = jnp.max(slot_counts[0].reshape(tiles, TILE), axis=1)
    row_low = jnp.min(block_row.reshape(NBR, tiles, TILE), axis=(0, 2))
    row_high = jnp.max(block_row.reshape(NBR, tiles, TILE), axis=(0, 2))
    rows = jnp.stack([row_low, row_high])
    pad = ((0, NPAD - NBR), (0, 0))
    index = jnp.pad(jnp.where(live, index, 0), pad)
    weight = jnp.pad(jnp.where(live, density_scale, 0.0).astype(f32), pad)
    centres8 = jnp.pad(centres, ((0, 5), (0, 0)))

    dens_one = density_call(1, counts, rows, radial_one, table_one, centres8, index, weight)
    factors_one, invariants_one = contract(dens_one, coupling_one)
    chosen_one = jnp.dot(coefficient_one.T, onehot, precision=highest)
    energy_one = jnp.sum(invariants_one * chosen_one, axis=0)
    features, features_back = jax.vjp(feature_map, invariants_one, mixing)
    feat_left, feat_right = shift_pair(features, "dom")
    feat_ext = jnp.stack([feat_left, features, feat_right], axis=1)
    table_two = jnp.concatenate(
        [table_one[: 3 * 3 * tiles], feat_ext.reshape(SPECIES * 3 * tiles, TILE)], axis=0
    )
    dens_two = density_call(2, counts, rows, radial_two, table_two, centres8, index, weight)
    factors_two, invariants_two = contract(dens_two, coupling_two)
    chosen_two = jnp.dot(coefficient_two.T, onehot, precision=highest)
    site_energy = energy_one + jnp.sum(invariants_two * chosen_two, axis=0)
    structure_ids = structure[0]
    slots_total = target_energy.shape[1]
    energy_part = jax.ops.segment_sum(site_energy, structure_ids, num_segments=slots_total)
    count_part = jax.ops.segment_sum(onehot.T, structure_ids, num_segments=slots_total)
    energy_sum, species_count = lax.psum((energy_part, count_part), "dom")
    atom_total = jnp.maximum(jnp.sum(species_count, axis=1), 1.0)
    fraction = species_count / atom_total[:, None]
    gram_part = jnp.dot(fraction.T, fraction, precision=highest)
    right_part = jnp.dot(fraction.T, target_energy[0], precision=highest)
    gram_matrix, right_side = lax.psum((gram_part, right_part), "grp")
    offsets = small_solve(gram_matrix + ridge_weight * jnp.eye(SPECIES, dtype=f32), right_side)
    energies = energy_sum / atom_total + jnp.dot(fraction, offsets, precision=highest)

    def unpack(window, own):
        spread = window.reshape(NVAL, 32, TILE)[:, : 3 * tiles].reshape(NVAL, 3, atoms)
        return spread

    grad_dens_two = contract_back(factors_two, chosen_two, coupling_two)
    window_two, own_two, rgr_two = backward_call(
        2, counts, rows, radial_two, table_two, centres8, index, weight, grad_dens_two
    )
    spread_two = unpack(window_two, own_two)
    feat_spread = spread_two[3:]
    from_right = lax.ppermute(
        feat_spread[:, 0], "dom", [(i + 1, i) for i in range(lax.axis_size("dom") - 1)]
    )
    from_left = lax.ppermute(
        feat_spread[:, 2], "dom", [(i, i + 1) for i in range(lax.axis_size("dom") - 1)]
    )
    grad_features = feat_spread[:, 1] + from_right + from_left
    coefficient_second = jnp.dot(onehot, invariants_two.T, precision=highest)
    grad_invariants, mixing_gradient = features_back(grad_features)
    grad_dens_one = contract_back(factors_one, chosen_one + grad_invariants, coupling_one)
    window_one, own_one, rgr_one = backward_call(
        1, counts, rows, radial_one, table_one, centres8, index, weight, grad_dens_one
    )
    spread_one = unpack(window_one, own_one)
    coefficient_first = jnp.dot(onehot, invariants_one.T, precision=highest)
    pos_spread = spread_one[:3] + spread_two[:3]
    pos_right = lax.ppermute(
        pos_spread[:, 0], "dom", [(i + 1, i) for i in range(lax.axis_size("dom") - 1)]
    )
    pos_left = lax.ppermute(
        pos_spread[:, 2], "dom", [(i, i + 1) for i in range(lax.axis_size("dom") - 1)]
    )
    forces = (own_one[:3] + own_two[:3]) - pos_spread[:, 1] - pos_right - pos_left

    def radial_sum(partial_grad):
        return jnp.sum(partial_grad.reshape(NMAX, NRAD, 8 * TILE), axis=2)

    radial_first, coefficient_first, mixing_gradient, radial_second, coefficient_second = lax.psum(
        (
            radial_sum(rgr_one),
            coefficient_first,
            mixing_gradient,
            radial_sum(rgr_two),
            coefficient_second,
        ),
        ("dom", "grp"),
    )
    return (
        energies[None, :],
        offsets,
        forces[:, None, :],
        radial_first,
        coefficient_first,
        mixing_gradient,
        radial_second,
        coefficient_second,
    )


def solution(mesh):
    in_specs = (
        P(None, "grp", "dom"),
        P("grp", "dom"),
        P(None, "grp", "dom"),
        P("grp", "dom"),
        P("grp", "dom"),
        P("grp", None),
        P(),
        P(),
        P(),
        P(),
        P(),
        P(),
        P(),
    )
    out_specs = (P("grp", None), P(), P(None, "grp", "dom"), P(), P(), P(), P(), P())
    return jax.shard_map(
        per_device, mesh=mesh, in_specs=in_specs, out_specs=out_specs, check_vma=False
    )
```

time: 2280 us -> 842 us (0.37)
  other arithmetic: 922 us -> 23.8 us
  local copies, waits for them, and re-layouts: 815 us -> 10.8 us
  Pallas kernels: 0 us -> 567 us
  matrix products: 386 us -> 73.1 us
    scatter-add x3 -> x0, other arithmetic: 761 us -> none  [the longest x2 499 us: layer_density(): sites_all[:, slot_index]]
    pallas_call x0 -> x4, Pallas kernels: none -> 567 us  [the longest x2 448 us: backward_call(): pl.pallas_call(partial(backward_kernel, layer), out_shape=(jax.ShapeDtype...]
    gather x4 -> x0, local copies, waits for them, and re-layouts: 509 us -> none  [the longest x2 329 us: layer_density(): weights_all[:, slot_index]]
    dot_general x16 -> x4, matrix products: 361 us -> 49.4 us  [the longest x2 26.9 us: contract_back(): jnp.einsum('vdq,vqa->da', coupling, rounded, preferred_element_type=f32)]
    mul x7 -> x0, local copies, waits for them, and re-layouts: 78.2 us -> none  [the longest x3 44.1 us: densities(): weighted = channel_weight * (live_slots * density_scale)]
    transpose x4 -> x0, local copies, waits for them, and re-layouts: 60.5 us -> none  [densities(): jnp.einsum('mka,lka->mla', mixed_terms, angular, precision=highest)]
    mul x8 -> x0, other arithmetic: 49.8 us -> none  [the longest x4 36.9 us: densities(): weighted = channel_weight * (live_slots * density_scale)]
    dot_general x4 -> x0, local copies, waits for them, and re-layouts: 44.1 us -> none  [the longest x2 38.1 us: densities(): jnp.einsum('mka,lka->mla', mixed_terms, angular, precision=highest)]
  transfers between devices with their start and end apart: 10 -> 8, of which waited for: 0 -> 1; matrix products, arithmetic and copies ran while one was open for 10% -> 3% of each run, Pallas kernels for 0% -> 0%
where the time goes in v1:
time: 842 us; the launch traced here: 833 us
  Pallas kernels  567 us (67%)
  blocking collectives  108 us (13%)
  matrix products  73.1 us (9%)
  starting transfers between devices  27.9 us (3%)
  other arithmetic  23.8 us (3%)
  between operations  20.4 us (2%)
  local copies, waits for them, and re-layouts  10.8 us (1%)
    pallas_call x2, Pallas kernels, backward_call(): pl.pallas_call(partial(backward_kernel, layer), out_shape=(jax.ShapeDtype...  448 us
    pallas_call x2, Pallas kernels, density_call(): pl.pallas_call(partial(density_kernel, layer), out_shape=jax.ShapeDtypeSt...  119 us
    psum x1, blocking collectives, per_device(): energy_sum, species_count = lax.psum((energy_part, count_part), 'dom')  64.1 us
    psum x1, blocking collectives, per_device(): lax.psum((radial_sum(rgr_one), coefficient_first, mixing_gradient, radial...  39.3 us
    dot_general x2, matrix products, contract_back(): jnp.einsum('vdq,vqa->da', coupling, rounded, preferred_element_type=f32)  26.9 us
    dot_general x2, matrix products, contract(): jnp.einsum('vdq,da->vqa', coupling, dens_in, preferred_element_type=f32)  22.6 us
  transfers between devices with their start and end apart: 8, of which 1 were waited for; matrix products, arithmetic and copies ran while one was open for 3% of the time, Pallas kernels for 0%

profile of v1, /device:TPU:0, one launch (start us, length us, event | category | flops | bytes accessed | tf_op | source)
XLA Modules:
  0.0 832.5 jit_solution(5739394431723539898)
XLA Ops:
  0.6 0.0 copy-start
  0.7 0.7 copy.100
  1.4 0.7 convert_element_type.15
  2.1 1.3 collective-permute-start.1
  3.4 3.0 collective-permute-start
  6.5 0.7 fusion.47
  7.2 1.0 bitcast_select_fusion
  8.2 1.1 fusion.81
  9.3 0.1 bitcast_reduce_fusion
  9.5 0.8 reduce_max.21.cnt_ref
  10.3 8.3 scatter_custom_fusion.1
  18.7 0.0 collective-permute-done
  18.8 59.1 %density_1.1 = bf16[1960,1024]{1,0:T(8,128)(2,1)S(1)} custom-call(s32[8]{0:T(128)S(1)} %reduce_max.21.cnt_ref, s32[2,8]{1,0:T(2,128)S(1)} %pad_add_fusion.row_ref, f32[10,12]{1,0:T(8,128)S(1)} %copy-done.3, f32[96,128]{1,0:T(8,128)S(1)} %reshape.171.tab_ref, f32[8,1024]{1,0:T(8,128)S(1)} %pad.12.cen_ref, s32[64,1024]{1,0:T(8,128)S(1)} %pad.13.idx_ref, ...), custom_call_target="tpu_custom_call" | custom-call | tf_op jit(solution)/shard_map/density_1/pallas_call | solution.py:243
  77.8 0.0 copy-start.5
  77.9 0.0 copy-start.7
  77.9 11.3 %fusion.18 = f32[4,512,1024]{2,1,0:T(8,128)S(1)} fusion(bf16[4,1960,512]{2,1,0:T(8,128)(2,1)} %param.20, bf16[1960,1024]{1,0:T(8,128)(2,1)S(1)} %density_1.1), kind=kOutput, calls=%fused_computation.22 | convolution fusion | flops 8220835840 | bytes 20430848 | tf_op jit(solution)/shard_map/vdq,da->vqa/dot_general | solution.py:525
  89.2 3.2 copy-done.4
  92.4 2.8 multiply_reduce_fusion
  95.2 1.2 broadcast_multiply_fusion
  96.4 4.9 collective-permute-start.2
  101.3 1.5 collective-permute-start.3
  103.0 1.4 collective-permute-done.3
  104.5 59.7 %density_2.1 = bf16[1960,1024]{1,0:T(8,128)(2,1)S(1)} custom-call(s32[8]{0:T(128)S(1)} %reduce_max.21.cnt_ref, s32[2,8]{1,0:T(2,128)S(1)} %pad_add_fusion.row_ref, f32[10,12]{1,0:T(8,128)S(1)} %copy-done.2, f32[168,128]{1,0:T(8,128)S(1)} %constant_dynamic-update-slice_fusion.tab_ref, f32[8,1024]{1,0:T(8,128)S(1)} %pad.12.cen_ref, ...), custom_call_target="tpu_custom_call" | custom-call | tf_op jit(solution)/shard_map/density_2/pallas_call | solution.py:243
  164.3 11.3 %fusion.21 = f32[4,512,1024]{2,1,0:T(8,128)S(1)} fusion(bf16[4,1960,512]{2,1,0:T(8,128)(2,1)} %param.24, bf16[1960,1024]{1,0:T(8,128)(2,1)S(1)} %density_2.1), kind=kOutput, calls=%fused_computation.23 | convolution fusion | flops 8220835840 | bytes 20430848 | tf_op jit(solution)/shard_map/vdq,da->vqa/dot_general | solution.py:525
  175.6 0.0 copy-start.9
  175.6 4.0 fusion.40
  179.6 7.7 scatter_custom_fusion
  187.3 64.1 %all-reduce.4 = (f32[512,4]{1,0:T(8,128)}, f32[512]{0:T(512)S(1)}) all-reduce(f32[512,4]{1,0:T(8,128)S(1)} %scatter_custom_fusion.1, f32[512]{0:T(512)S(1)} %scatter_custom_fusion), channel_id=1, replica_groups=mesh['dom'=16,'grp'=2] {'dom'}, use_global_device_ids=true, to_apply=%region_11.12 | all-reduce | flops 2560 | bytes 20480 | tf_op jit(solution)/shard_map/psum | solution.py:607
  251.5 1.1 reduce_sum.70
  252.6 1.7 fusion.80
  254.3 1.3 convolution_bitcast_fusion.3
  255.6 1.1 fusion.57
  256.7 4.9 all-reduce.5
  261.6 0.6 fusion.85
  266.2 0.6 fusion.88
  268.2 0.6 fusion.86
  268.8 0.6 slice.218
  269.4 0.6 slice.224
  273.8 14.0 %convolution_bitcast_fusion.1.dd_ref = f32[1960,1024]{1,0:T(8,128)} fusion(bf16[4,1960,512]{2,1,0:T(8,128)(2,1)} %param.24, bf16[1,512,1024]{2,1,0:T(8,128)(2,1)} %get-tuple-element.75, bf16[1,512,1024]{2,1,0:T(8,128)(2,1)} %get-tuple-element.76, bf16[1,512,1024]{2,1,0:T(8,128)(2,1)} %get-tuple-element.77, bf16[1,512,1024]{2,1,0:T(8,128)(2,1)} %get-tuple-element.74), kind=kOutput, calls=%fused_computation.3 | convolution fusion | flops 8227127296 | bytes 20250624 | tf_op jit(solution)/shard_map/vdq,vqa->da/dot_general | solution.py:542
  287.8 225.7 %backward_2.1 = (f32[224,128]{1,0:T(8,128)S(1)}, f32[8,1024]{1,0:T(8,128)S(1)}, f32[960,128]{1,0:T(8,128)S(1)}) custom-call(s32[8]{0:T(128)S(1)} %reduce_max.21.cnt_ref, s32[2,8]{1,0:T(2,128)S(1)} %pad_add_fusion.row_ref, f32[10,12]{1,0:T(8,128)S(1)} %copy-done.2, f32[168,128]{1,0:T(8,128)S(1)} %constant_dynamic-update-slice_fusion.tab_ref, ...), custom_call_target="tpu_custom_call" | custom-call | tf_op jit(solution)/shard_map/backward_2/pallas_call | solution.py:466
  513.6 1.3 collective-permute-start.4
  514.9 11.0 %collective-permute-start.5 = (f32[4,1024]{1,0:T(4,128)S(1)}, f32[4,1024]{1,0:T(4,128)S(1)}, u32[]{:S(2)}, u32[]{:S(2)}) collective-permute-start(f32[4,1024]{1,0:T(4,128)S(1)} %bitcast.327), channel_id=1, source_target_pairs={{0,2},{2,4},{4,6},{6,8},{8,10},{10,12},{12,14},{14,16},{16,18},{18... | collective-permute-start | bytes 49160 | tf_op jit(solution)/shard_map/ppermute | solution.py:629
  525.9 2.6 fusion.56
  528.5 0.7 fusion.87
  529.2 0.6 slice.225
  531.2 0.6 slice.243
  540.3 0.1 pad_maximum_fusion.3
  540.3 1.4 fusion.76
  541.7 0.6 divide_add_fusion
  542.3 1.0 reshape.176
  543.3 1.2 reduce_sum.73
  544.5 0.0 collective-permute-done.4
  544.6 5.6 fusion.36
  550.2 12.9 %convolution_bitcast_fusion.dd_ref = f32[1960,1024]{1,0:T(8,128)} fusion(bf16[4,1960,512]{2,1,0:T(8,128)(2,1)} %param.20, bf16[1,512,1024]{2,1,0:T(8,128)(2,1)S(1)} %get-tuple-element.71, bf16[1,512,1024]{2,1,0:T(8,128)(2,1)S(1)} %get-tuple-element.72, bf16[1,512,1024]{2,1,0:T(8,128)(2,1)S(1)} %get-tuple-element.73, ...), kind=kOutput, calls=%fused_computation.2 | convolution fusion | flops 8227127296 | bytes 20250624 | tf_op jit(solution)/shard_map/vdq,vqa->da/dot_general | solution.py:542
  563.1 222.2 %backward_1.1 = (f32[224,128]{1,0:T(8,128)S(1)}, f32[8,1024]{1,0:T(8,128)S(1)}, f32[960,128]{1,0:T(8,128)S(1)}) custom-call(s32[8]{0:T(128)S(1)} %reduce_max.21.cnt_ref, s32[2,8]{1,0:T(2,128)S(1)} %pad_add_fusion.row_ref, f32[10,12]{1,0:T(8,128)S(1)} %copy-done.3, f32[96,128]{1,0:T(8,128)S(1)} %reshape.171.tab_ref, f32[8,1024]{1,0:T(8,128)S(1)} %pad.12.cen_ref, ...), custom_call_target="tpu_custom_call" | custom-call | tf_op jit(solution)/shard_map/backward_1/pallas_call | solution.py:466
  785.4 0.0 copy-start.1
  785.4 1.3 collective-permute-start.6
  786.8 3.6 collective-permute-start.7
  790.3 1.9 fusion.60
  792.2 0.1 reshape.175
  792.3 0.1 reduce_sum.72
  792.4 39.3 %all-reduce.3 = (f32[10,12]{1,0:T(8,128)}, f32[4,512]{1,0:T(4,128)}, f32[512,4]{0,1:T(4,128)}, f32[10,12]{1,0:T(8,128)}, f32[4,512]{1,0:T(4,128)}) all-reduce(f32[10,12]{1,0:T(8,128)S(1)} %reduce_sum.72, f32[4,512]{1,0:T(4,128)S(1)} %fusion.57, f32[512,4]{0,1:T(4,128)S(1)} %fusion.60, ...), channel_id=1, replica_groups=mesh['dom'=16,'grp'=2] {'dom','grp'}, use_global_device_ids=true, to_apply=%region_17.18 | all-reduce | flops 6384 | bytes 51072 | tf_op jit(solution)/shard_map/psum | solution.py:653
  831.7 0.0 collective-permute-done.6
  831.7 0.6 copy.61
  (55 shorter events, 0.6 us)
Async XLA Ops:
  0.6 174.9 %copy-start = (f32[4,512]{1,0:T(4,128)S(1)}, f32[4,512]{1,0:T(4,128)}, u32[]{:S(2)}) copy-start(f32[4,512]{1,0:T(4,128)} %param.25) | copy-start | bytes 24580
  0.6 18.1 %copy-start.3 = (f32[10,12]{1,0:T(8,128)S(1)}, f32[10,12]{1,0:T(8,128)}, u32[]{:S(2)}) copy-start(f32[10,12]{1,0:T(8,128)} %rad_ref.7) | copy-start | bytes 1444
  2.1 16.6 %collective-permute-start.1 = (f32[4,1024]{1,0:T(4,128)S(1)}, f32[4,1024]{1,0:T(4,128)S(1)}, u32[]{:S(2)}, u32[]{:S(2)}) collective-permute-start(f32[4,1024]{1,0:T(4,128)S(1)} %pad_maximum_fusion.2), channel_id=1, source_target_pairs={{2,0},{4,2},{6,4},{8,6},{10,8},{12,10},{14,12},{16,14},{18,16},{20... | collective-permute-start | bytes 49160 | tf_op jit(solution)/shard_map/ppermute | solution.py:38
  3.4 15.3 %collective-permute-start = (f32[4,1024]{1,0:T(4,128)S(1)}, f32[4,1024]{1,0:T(4,128)S(1)}, u32[]{:S(2)}, u32[]{:S(2)}) collective-permute-start(f32[4,1024]{1,0:T(4,128)S(1)} %pad_maximum_fusion.2), channel_id=1, source_target_pairs={{0,2},{2,4},{4,6},{6,8},{8,10},{10,12},{12,14},{14,16},{16,18},{18... | collective-permute-start | bytes 49160 | tf_op jit(solution)/shard_map/ppermute | solution.py:37
  77.8 14.5 %copy-start.5 = (s32[1,1024]{1,0:T(1,128)S(1)}, s32[1,1024]{1,0:T(1,128)}, u32[]{:S(2)}) copy-start(s32[1,1024]{1,0:T(1,128)} %param.14) | copy-start | bytes 12292
  77.9 14.5 %copy-start.7 = (f32[4,512]{1,0:T(4,128)S(1)}, f32[4,512]{1,0:T(4,128)}, u32[]{:S(2)}) copy-start(f32[4,512]{1,0:T(4,128)} %param.21) | copy-start | bytes 24580
  89.2 3.2 copy-start.4
  92.4 2.8 copy-start.6
  95.2 9.4 %copy-start.2 = (f32[10,12]{1,0:T(8,128)S(1)}, f32[10,12]{1,0:T(8,128)}, u32[]{:S(2)}) copy-start(f32[10,12]{1,0:T(8,128)} %rad_ref.6) | copy-start | bytes 1444
  96.4 6.6 collective-permute-start.2
  101.3 3.1 collective-permute-start.3
  175.6 78.8 %copy-start.9 = (f32[1,512]{1,0:T(1,128)S(1)}, f32[1,512]{1,0:T(1,128)}, u32[]{:S(2)}) copy-start(f32[1,512]{1,0:T(1,128)} %param.18) | copy-start | bytes 6148
  513.6 30.9 %collective-permute-start.4 = (f32[4,1024]{1,0:T(4,128)S(1)}, f32[4,1024]{1,0:T(4,128)S(1)}, u32[]{:S(2)}, u32[]{:S(2)}) collective-permute-start(f32[4,1024]{1,0:T(4,128)S(1)} %bitcast.326), channel_id=1, source_target_pairs={{2,0},{4,2},{6,4},{8,6},{10,8},{12,10},{14,12},{16,14},{18,16},{20... | collective-permute-start | bytes 49160 | tf_op jit(solution)/shard_map/ppermute | solution.py:626
  514.9 29.6 %collective-permute-start.5 = (f32[4,1024]{1,0:T(4,128)S(1)}, f32[4,1024]{1,0:T(4,128)S(1)}, u32[]{:S(2)}, u32[]{:S(2)}) collective-permute-start(f32[4,1024]{1,0:T(4,128)S(1)} %bitcast.327), channel_id=1, source_target_pairs={{0,2},{2,4},{4,6},{6,8},{8,10},{10,12},{12,14},{14,16},{16,18},{18... | collective-permute-start | bytes 49160 | tf_op jit(solution)/shard_map/ppermute | solution.py:629
  540.3 9.9 %copy-start.8 = (f32[4]{0:T(128)}, f32[4]{0:T(128)S(1)}, u32[]{:S(2)}) copy-start(f32[4]{0:T(128)S(1)} %pad_maximum_fusion.3) | copy-start | bytes 52
  785.4 46.9 %copy-start.1 = (f32[4,512]{1,0:T(4,128)S(1)}, f32[4,512]{1,0:T(4,128)}, u32[]{:S(2)}) copy-start(f32[4,512]{1,0:T(4,128)} %param.25) | copy-start | bytes 24580
  785.4 46.2 %collective-permute-start.6 = (f32[3,1024]{1,0:T(4,128)S(1)}, f32[3,1024]{1,0:T(4,128)S(1)}, u32[]{:S(2)}, u32[]{:S(2)}) collective-permute-start(f32[3,1024]{1,0:T(4,128)S(1)} %bitcast.324), channel_id=1, source_target_pairs={{2,0},{4,2},{6,4},{8,6},{10,8},{12,10},{14,12},{16,14},{18,16},{20... | collective-permute-start | bytes 36872 | tf_op jit(solution)/shard_map/ppermute | solution.py:642
  786.8 44.9 %collective-permute-start.7 = (f32[3,1024]{1,0:T(4,128)S(1)}, f32[3,1024]{1,0:T(4,128)S(1)}, u32[]{:S(2)}, u32[]{:S(2)}) collective-permute-start(f32[3,1024]{1,0:T(4,128)S(1)} %bitcast.325), channel_id=1, source_target_pairs={{0,2},{2,4},{4,6},{6,8},{8,10},{10,12},{12,14},{14,16},{16,18},{18... | collective-permute-start | bytes 36872 | tf_op jit(solution)/shard_map/ppermute | solution.py:645
